TPU v7x, 8 devices: a whole 2x2x1 slice. The times are simulated.
8 devices in a mesh: ens: 2 (over z, y), feat: 4 (over x, core).
Axes of the slice: x: 2, y: 2, z: 1, core: 2. Of those that a mesh axis runs over, the one named last changes fastest.
Arguments:
- particles: float32 [1024, 32768], P('ens', 'feat'), parts along dimension 0
- prec_diag: float32 [65536], P(('ens', 'feat')), parts along dimension 0
- low_factor: bfloat16 [65536, 16], P(('ens', 'feat')), parts along dimension 0
- prior_mean: float32 [65536], P(('ens', 'feat')), parts along dimension 0
- data_mat: bfloat16 [2048, 32768], P('ens', 'feat'), parts along dimension 0
- labels: int32 [2048], P('ens'), parts along dimension 0
Outputs:
- output: float32 [1024, 32768], P('ens', 'feat'), parts along dimension 0
There are 2 independent parts. A program takes and returns all parts, laid end to end along the dimension named above; each array names one.
All inputs are finite; a program needn't handle non-finite values.
Results may differ from a plain program's by a relative error of at most 0.001.
Values are sent between devices in bfloat16 or wider.
A program may use at most 1 GiB of HBM per device.

v0:
```python
import math
import jax
import jax.numpy as jnp
from jax import lax
from jax.sharding import PartitionSpec as P

NUM_STEPS = 3
DIMS_NT = (((1,), (1,)), ((), ()))


def solution(mesh):
    feat_size = mesh.shape["feat"]

    def local_run(particles, prec_diag, low_factor, prior_mean, data_mat, labels):
        n_part, dim_local = particles.shape
        dim_full = dim_local * feat_size
        m_rows = data_mat.shape[0]
        band_width = 2.0 * dim_full
        step_size = dim_full / 4.0
        lik_weight = 2.0 / math.sqrt(m_rows * dim_full)
        targets = labels.astype(jnp.float32)[None, :]
        state = particles
        for step_idx in range(NUM_STEPS):
            part_bf = state.astype(jnp.bfloat16)
            centred = state - prior_mean
            projected = lax.psum(jnp.dot(centred.astype(jnp.bfloat16), low_factor, preferred_element_type=jnp.float32), "feat")
            gram_mat = lax.psum(lax.dot_general(part_bf, part_bf, DIMS_NT, preferred_element_type=jnp.float32), "feat")
            logits = lax.psum(lax.dot_general(part_bf, data_mat, DIMS_NT, preferred_element_type=jnp.float32), "feat")
            sq_norm = jnp.diagonal(gram_mat)
            sq_dist = jnp.maximum(sq_norm[:, None] + sq_norm[None, :] - 2.0 * gram_mat, 0.0)
            kernel = jnp.exp(-sq_dist / band_width)
            residual = targets - jax.nn.sigmoid(logits)
            low_rank = lax.dot_general(projected.astype(jnp.bfloat16), low_factor, DIMS_NT, preferred_element_type=jnp.float32)
            lik_term = jnp.dot(residual.astype(jnp.bfloat16), data_mat, preferred_element_type=jnp.float32)
            log_grad = lik_weight * lik_term - centred * prec_diag - low_rank
            kern_bf = kernel.astype(jnp.bfloat16)
            driving = jnp.dot(kern_bf, log_grad.astype(jnp.bfloat16), preferred_element_type=jnp.float32)
            pulled = jnp.dot(kern_bf, part_bf, preferred_element_type=jnp.float32)
            row_sum = jnp.sum(kernel, axis=1, keepdims=True)
            update_dir = (driving + (2.0 / band_width) * (row_sum * state - pulled)) / n_part
            state = state + step_size * update_dir
        return state

    return jax.shard_map(
        local_run,
        mesh=mesh,
        in_specs=(P("ens", "feat"), P(("ens", "feat")), P(("ens", "feat"), None),
                  P(("ens", "feat")), P("ens", "feat"), P("ens")),
        out_specs=P("ens", "feat"),
        check_vma=False,
    )
```

profile of v0, /device:TPU:0, one launch (start us, length us, event | category | flops | bytes accessed | tf_op | source)
XLA Modules:
  0.0 528.8 jit_solution(14759848376296177629)
XLA Ops:
  6.5 16.1 %fusion.40 = f32[512,512]{1,0:T(8,128)} fusion(f32[512,8192]{1,0:T(8,128)} %param.6), kind=kOutput, calls=%fused_computation.59 | convolution fusion | flops 4299161600 | bytes 17825792 | tf_op jit(solution)/shard_map/dot_general | solution.py:27
  22.6 18.2 %fusion.38 = f32[512,1024]{1,0:T(8,128)} fusion(bf16[1024,8192]{1,0:T(8,128)(2,1)} %param.10, f32[512,8192]{1,0:T(8,128)} %param.6), kind=kOutput, calls=%fused_computation.57 | convolution fusion | flops 8594128896 | bytes 35651584 | tf_op jit(solution)/shard_map/dot_general | solution.py:28
  40.9 0.0 all-reduce.9.cloned.1.call-start
  41.0 8.1 %fusion = f32[512,16]{1,0:T(8,128)S(1)} fusion(bf16[8192,16]{0,1:T(8,128)(2,1)S(1)} %copy-done, f32[512,8192]{1,0:T(8,128)} %param.6, f32[8192]{0:T(1024)S(1)} %copy-done.4), kind=kOutput, calls=%fused_computation.12 | convolution fusion | flops 142606336 | bytes 17104896 | tf_op jit(solution)/shard_map/dot_general | solution.py:26
  49.1 22.3 %psum.65 = bf16[512,16]{1,0:T(8,128)(2,1)S(1)} all-reduce(f32[512,16]{1,0:T(8,128)S(1)} %fusion), channel_id=1, replica_groups=mesh['ens'=2,'feat'=4] {'feat'}, use_global_device_ids=true, to_apply=%region_2.0 | all-reduce | flops 8192 | bytes 49152 | tf_op jit(solution)/shard_map/psum | solution.py:26
  71.4 8.5 %fusion.53 = f32[512,8192]{1,0:T(8,128)} fusion(bf16[512,16]{1,0:T(8,128)(2,1)S(1)} %psum.65, bf16[8192,16]{0,1:T(8,128)(2,1)S(1)} %copy-done), kind=kOutput, calls=%fused_computation.66 | convolution fusion | flops 134217728 | bytes 17055744 | tf_op jit(solution)/shard_map/dot_general | solution.py:33
  79.9 30.9 %all-reduce.11.cloned.1.call-done = (f32[512,1024]{1,0:T(8,128)}, f32[512,512]{1,0:T(8,128)}) async-done(((f32[512,1024]{1,0:T(8,128)}, f32[512,512]{1,0:T(8,128)}), (f32[512,1024]{1,0:T(8,128)}, f32[512,512]{1,0:T(8,128)})) %all-reduce.11.cloned.1.call-update) | async-done | bytes 3145744 | tf_op jit(solution)/shard_map/psum | solution.py:28
  110.8 8.7 %gather_fusion = f32[512]{0:T(512)S(1)} fusion(f32[512,512]{1,0:T(8,128)} %get-tuple-element.10, s32[512]{0:T(512)S(1)} %bitcast.31), kind=kCustom, calls=%fused_computation | custom fusion | bytes 8192 | tf_op jit(solution)/shard_map/jit(diagonal)/cond/branch_0_fun/gather | solution.py:29
  119.5 1.7 fusion.12
  121.2 28.9 %fusion.49 = f32[512,8192]{1,0:T(8,128)} fusion(f32[512,512]{1,0:T(8,128)} %get-tuple-element.10, f32[512]{0:T(512)S(1)} %gather_fusion, f32[512,8192]{1,0:T(8,128)} %fusion.53, f32[512,8192]{1,0:T(8,128)} %param.6, bf16[1024,8192]{1,0:T(8,128)(2,1)} %param.10, f32[8192]{0:T(1024)S(1)} %copy-done.6, f32[8192]{0:T(1024)S(1)} %copy-done.4, ...), kind=kOutput, calls=%fused_computation.63 | convolution fusion | flops 12914524160 | bytes 70326272 | tf_op jit(solution)/shard_map/dot_general | solution.py:37
  150.1 30.0 %multiply_add_fusion.2 = f32[512,8192]{1,0:T(8,128)} fusion(f32[512,8192]{1,0:T(8,128)} %param.6, f32[512,8192]{1,0:T(8,128)} %fusion.49, f32[512]{0:T(512)S(1)} %fusion.12, f32[512,512]{1,0:T(8,128)S(1)} %copy-done.1, f32[512]{0:T(512)S(1)} %gather_fusion), kind=kOutput, calls=%fused_computation.7 | convolution fusion | flops 4326162432 | bytes 51384320 | tf_op jit(solution)/shard_map/dot_general | solution.py:38
  180.1 18.6 %fusion.30 = f32[512,1024]{1,0:T(8,128)} fusion(bf16[1024,8192]{1,0:T(8,128)(2,1)} %param.10, f32[512,8192]{1,0:T(8,128)} %multiply_add_fusion.2), kind=kOutput, calls=%fused_computation.49 | convolution fusion | flops 8594128896 | bytes 35651584 | tf_op jit(solution)/shard_map/dot_general | solution.py:28
  198.7 16.1 %fusion.32 = f32[512,512]{1,0:T(8,128)} fusion(f32[512,8192]{1,0:T(8,128)} %multiply_add_fusion.2), kind=kOutput, calls=%fused_computation.51 | convolution fusion | flops 4299161600 | bytes 17825792 | tf_op jit(solution)/shard_map/dot_general | solution.py:27
  214.8 0.0 all-reduce.7.cloned.1.call-start
  214.9 8.1 %fusion.1 = f32[512,16]{1,0:T(8,128)S(1)} fusion(bf16[8192,16]{0,1:T(8,128)(2,1)S(1)} %copy-done, f32[512,8192]{1,0:T(8,128)} %multiply_add_fusion.2, f32[8192]{0:T(1024)S(1)} %copy-done.4), kind=kOutput, calls=%fused_computation.13 | convolution fusion | flops 142606336 | bytes 17104896 | tf_op jit(solution)/shard_map/dot_general | solution.py:26
  223.0 19.5 %psum.68 = bf16[512,16]{1,0:T(8,128)(2,1)S(1)} all-reduce(f32[512,16]{1,0:T(8,128)S(1)} %fusion.1), channel_id=1, replica_groups=mesh['ens'=2,'feat'=4] {'feat'}, use_global_device_ids=true, to_apply=%region_6.7 | all-reduce | flops 8192 | bytes 49152 | tf_op jit(solution)/shard_map/psum | solution.py:26
  242.5 8.0 %fusion.52 = f32[512,8192]{1,0:T(8,128)} fusion(bf16[512,16]{1,0:T(8,128)(2,1)S(1)} %psum.68, bf16[8192,16]{0,1:T(8,128)(2,1)S(1)} %copy-done), kind=kOutput, calls=%fused_computation.65 | convolution fusion | flops 134217728 | bytes 17055744 | tf_op jit(solution)/shard_map/dot_general | solution.py:33
  250.5 31.5 %all-reduce.9.cloned.1.call-done = (f32[512,1024]{1,0:T(8,128)}, f32[512,512]{1,0:T(8,128)}) async-done(((f32[512,1024]{1,0:T(8,128)}, f32[512,512]{1,0:T(8,128)}), (f32[512,1024]{1,0:T(8,128)}, f32[512,512]{1,0:T(8,128)})) %all-reduce.9.cloned.1.call-update) | async-done | bytes 3145744 | tf_op jit(solution)/shard_map/psum | solution.py:28
  282.0 8.6 %gather_fusion.1 = f32[512]{0:T(512)S(1)} fusion(f32[512,512]{1,0:T(8,128)} %get-tuple-element.8, s32[512]{0:T(512)S(1)} %bitcast.32), kind=kCustom, calls=%fused_computation.1 | custom fusion | bytes 8192 | tf_op jit(solution)/shard_map/jit(diagonal)/cond/branch_0_fun/gather | solution.py:29
  290.6 1.7 fusion.14
  292.3 28.9 %fusion.46 = f32[512,8192]{1,0:T(8,128)} fusion(f32[512,512]{1,0:T(8,128)} %get-tuple-element.8, f32[512]{0:T(512)S(1)} %gather_fusion.1, f32[512,8192]{1,0:T(8,128)} %fusion.52, f32[512,8192]{1,0:T(8,128)} %multiply_add_fusion.2, bf16[1024,8192]{1,0:T(8,128)(2,1)} %param.10, f32[8192]{0:T(1024)S(1)} %copy-done.6, f32[8192]{0:T(1024)S(1)} %copy-done.4, ...), kind=kOutput, calls=%fused_computation.62 | convolution fusion | flops 12914524160 | bytes 70326272 | tf_op jit(solution)/shard_map/dot_general | solution.py:37
  321.2 29.8 %multiply_add_fusion.1 = f32[512,8192]{1,0:T(8,128)} fusion(f32[512,8192]{1,0:T(8,128)} %multiply_add_fusion.2, f32[512,8192]{1,0:T(8,128)} %fusion.46, f32[512]{0:T(512)S(1)} %fusion.14, f32[512,512]{1,0:T(8,128)S(1)} %copy-done.2, f32[512]{0:T(512)S(1)} %gather_fusion.1), kind=kOutput, calls=%fused_computation.5 | convolution fusion | flops 4326162432 | bytes 51384320 | tf_op jit(solution)/shard_map/dot_general | solution.py:38
  351.0 18.4 %fusion.25 = f32[512,1024]{1,0:T(8,128)} fusion(bf16[1024,8192]{1,0:T(8,128)(2,1)} %param.10, f32[512,8192]{1,0:T(8,128)} %multiply_add_fusion.1), kind=kOutput, calls=%fused_computation.44 | convolution fusion | flops 8594128896 | bytes 35651584 | tf_op jit(solution)/shard_map/dot_general | solution.py:28
  369.5 16.0 %fusion.27 = f32[512,512]{1,0:T(8,128)} fusion(f32[512,8192]{1,0:T(8,128)} %multiply_add_fusion.1), kind=kOutput, calls=%fused_computation.46 | convolution fusion | flops 4299161600 | bytes 17825792 | tf_op jit(solution)/shard_map/dot_general | solution.py:27
  385.5 8.1 %fusion.2 = f32[512,16]{1,0:T(8,128)S(1)} fusion(bf16[8192,16]{0,1:T(8,128)(2,1)S(1)} %copy-done, f32[512,8192]{1,0:T(8,128)} %multiply_add_fusion.1, f32[8192]{0:T(1024)S(1)} %copy-done.4), kind=kOutput, calls=%fused_computation.14 | convolution fusion | flops 142606336 | bytes 17104896 | tf_op jit(solution)/shard_map/dot_general | solution.py:26
  393.6 19.6 %psum.71 = bf16[512,16]{1,0:T(8,128)(2,1)S(1)} all-reduce(f32[512,16]{1,0:T(8,128)S(1)} %fusion.2), channel_id=1, replica_groups=mesh['ens'=2,'feat'=4] {'feat'}, use_global_device_ids=true, to_apply=%region_10.11 | all-reduce | flops 8192 | bytes 49152 | tf_op jit(solution)/shard_map/psum | solution.py:26
  413.2 8.5 %fusion.51 = f32[512,8192]{1,0:T(8,128)} fusion(bf16[512,16]{1,0:T(8,128)(2,1)S(1)} %psum.71, bf16[8192,16]{0,1:T(8,128)(2,1)S(1)} %copy-done), kind=kOutput, calls=%fused_computation.64 | convolution fusion | flops 134217728 | bytes 17055744 | tf_op jit(solution)/shard_map/dot_general | solution.py:33
  421.7 31.0 %all-reduce.7.cloned.1.call-done = (f32[512,1024]{1,0:T(8,128)}, f32[512,512]{1,0:T(8,128)}) async-done(((f32[512,1024]{1,0:T(8,128)}, f32[512,512]{1,0:T(8,128)}), (f32[512,1024]{1,0:T(8,128)}, f32[512,512]{1,0:T(8,128)})) %all-reduce.7.cloned.1.call-update) | async-done | bytes 3145744 | tf_op jit(solution)/shard_map/psum | solution.py:28
  452.7 8.6 %gather_fusion.2 = f32[512]{0:T(512)S(1)} fusion(f32[512,512]{1,0:T(8,128)} %get-tuple-element.6, s32[512]{0:T(512)S(1)} %bitcast.33), kind=kCustom, calls=%fused_computation.2 | custom fusion | bytes 8192 | tf_op jit(solution)/shard_map/jit(diagonal)/cond/branch_0_fun/gather | solution.py:29
  461.3 1.7 fusion.16
  463.0 28.9 %fusion.43 = f32[512,8192]{1,0:T(8,128)} fusion(f32[512,512]{1,0:T(8,128)} %get-tuple-element.6, f32[512]{0:T(512)S(1)} %gather_fusion.2, f32[512,8192]{1,0:T(8,128)} %fusion.51, f32[512,8192]{1,0:T(8,128)} %multiply_add_fusion.1, bf16[1024,8192]{1,0:T(8,128)(2,1)} %param.10, f32[8192]{0:T(1024)S(1)} %copy-done.6, f32[8192]{0:T(1024)S(1)} %copy-done.4, ...), kind=kOutput, calls=%fused_computation.61 | convolution fusion | flops 12914524160 | bytes 70326272 | tf_op jit(solution)/shard_map/dot_general | solution.py:37
  491.9 30.0 %multiply_add_fusion = f32[512,8192]{1,0:T(8,128)} fusion(f32[512,8192]{1,0:T(8,128)} %multiply_add_fusion.1, f32[512,8192]{1,0:T(8,128)} %fusion.43, f32[512]{0:T(512)S(1)} %fusion.16, f32[512,512]{1,0:T(8,128)S(1)} %copy-done.3, f32[512]{0:T(512)S(1)} %gather_fusion.2), kind=kOutput, calls=%fused_computation.3 | convolution fusion | flops 4326162432 | bytes 51384320 | tf_op jit(solution)/shard_map/dot_general | solution.py:38
  (20 shorter events, 0.1 us)
Async XLA Ops:
  6.5 34.4 %copy-start = (bf16[8192,16]{0,1:T(8,128)(2,1)S(1)}, bf16[8192,16]{0,1:T(8,128)(2,1)}, u32[]{:S(2)}) copy-start(bf16[8192,16]{0,1:T(8,128)(2,1)} %param.8) | copy-start | bytes 786436
  6.5 104.3 %all-reduce.11.cloned.1.call-start = ((), (), s32[]{:S(2)}) async-start(), calls=%async_computation.2 | async-start | bytes 6291456 | tf_op jit(solution)/shard_map/psum | solution.py:28
  22.6 18.3 %copy-start.5 = (s32[1024]{0:T(1024)S(1)}, s32[1024]{0:T(1024)}, u32[]{:S(2)}) copy-start(s32[1024]{0:T(1024)} %param.11) | copy-start | bytes 12292
  22.6 18.4 %copy-start.4 = (f32[8192]{0:T(1024)S(1)}, f32[8192]{0:T(1024)}, u32[]{:S(2)}) copy-start(f32[8192]{0:T(1024)} %param.9) | copy-start | bytes 98308
  40.9 241.1 %all-reduce.9.cloned.1.call-start = ((), (), s32[]{:S(2)}) async-start(), calls=%async_computation.1 | async-start | bytes 6291456 | tf_op jit(solution)/shard_map/psum | solution.py:28
  49.1 72.1 %copy-start.6 = (f32[8192]{0:T(1024)S(1)}, f32[8192]{0:T(1024)}, u32[]{:S(2)}) copy-start(f32[8192]{0:T(1024)} %param.7) | copy-start | bytes 98308
  121.2 28.9 %copy-start.1 = (f32[512,512]{1,0:T(8,128)S(1)}, f32[512,512]{1,0:T(8,128)}, u32[]{:S(2)}) copy-start(f32[512,512]{1,0:T(8,128)} %get-tuple-element.10) | copy-start | bytes 3145732
  214.8 237.9 %all-reduce.7.cloned.1.call-start = ((), (), s32[]{:S(2)}) async-start(), calls=%async_computation | async-start | bytes 6291456 | tf_op jit(solution)/shard_map/psum | solution.py:28
  292.3 28.9 %copy-start.2 = (f32[512,512]{1,0:T(8,128)S(1)}, f32[512,512]{1,0:T(8,128)}, u32[]{:S(2)}) copy-start(f32[512,512]{1,0:T(8,128)} %get-tuple-element.8) | copy-start | bytes 3145732
  463.0 28.9 %copy-start.3 = (f32[512,512]{1,0:T(8,128)S(1)}, f32[512,512]{1,0:T(8,128)}, u32[]{:S(2)}) copy-start(f32[512,512]{1,0:T(8,128)} %get-tuple-element.6) | copy-start | bytes 3145732
Sparse Core Ops, SparseCore 0:
  41.0 69.7 all-reduce.10
  214.9 67.0 all-reduce.8
  385.7 67.0 all-reduce.6
where the time goes:
time: 537 us; the launch traced here: 529 us
  matrix products  329 us (61%)
  waiting for transfers between devices  93.5 us (17%)
  blocking collectives  61.4 us (11%)
  local copies, waits for them, and re-layouts  26 us (5%)
  between operations  13.7 us (3%)
    psum x3, waiting for transfers between devices, local_run(): lax.psum(lax.dot_general(part_bf, data_mat, DIMS_NT, preferred_element_ty...  93.4 us
    dot_general x3, matrix products, local_run(): pulled = jnp.dot(kern_bf, part_bf, preferred_element_type=jnp.float32)  89.8 us
    dot_general x3, matrix products, local_run(): jnp.dot(kern_bf, log_grad.astype(jnp.bfloat16), preferred_element_type=jn...  86.7 us
    psum x3, blocking collectives, local_run(): lax.psum(jnp.dot(centred.astype(jnp.bfloat16), low_factor, preferred_elem...  61.4 us
    dot_general x3, matrix products, local_run(): lax.dot_general(part_bf, data_mat, DIMS_NT, preferred_element_type=jnp.fl...  55.3 us
    dot_general x3, matrix products, local_run(): lax.dot_general(part_bf, part_bf, DIMS_NT, preferred_element_type=jnp.flo...  48.2 us
    gather x3, local copies, waits for them, and re-layouts, local_run(): sq_norm = jnp.diagonal(gram_mat)  26 us
    dot_general x3, matrix products, local_run(): lax.dot_general(projected.astype(jnp.bfloat16), low_factor, DIMS_NT, pref...  25 us
  transfers between devices with their start and end apart: 3, of which 3 were waited for; matrix products, arithmetic and copies ran while one was open for 9% of the time, Pallas kernels for 0%

commit v1 on v0

v1 whole, which is shorter than its diff:
```python
import functools
import math
import jax
import jax.numpy as jnp
from jax import lax
from jax.experimental import pallas as pl
from jax.experimental.pallas import tpu as pltpu
from jax.sharding import PartitionSpec as P

NUM_STEPS = 3
NT = (((1,), (1,)), ((), ()))
F32 = jnp.float32
BF16 = jnp.bfloat16
N = 512
HB = 256
D = 8192
M = 1024
CW = 2048
SW = 512
NC = D // CW
VMEM_LIMIT = 67_043_328


def run_kernel(consts, th_hbm, lam_ref, ut_ref, mu_ref, a_hbm, y_ref,
               th_out, s_out, k_out, kv_out,
               th, a, tb, sbuf, zbuf, ra, snd, rb, rbuf, kx, kv, qacc, qall, dgs, dall, qt,
               ld_sem, a_sem, out_sem, as_sem, ar_sem, bs_sem, br_sem, cs_sem, cr_sem, ds_sem, dr_sem,
               ks_sem, kr_sem, ls_sem, lr_sem, qs_sem, qr_sem, gs_sem, gr_sem):
    lik_weight, inv_band, two_over_band, gain = consts
    me = lax.axis_index("feat")
    xx = me // 2
    cc = me % 2
    sib = xx * 2 + (1 - cc)
    far = (1 - xx) * 2 + cc
    diag_dev = (1 - xx) * 2 + (1 - cc)

    def rows_of(idx):
        return jnp.where(idx < 4, idx // 2, idx - 4) * HB

    def remote(src, dst, ssem, rsem, dev):
        return pltpu.make_async_remote_copy(
            src_ref=src, dst_ref=dst, send_sem=ssem, recv_sem=rsem,
            device_id={"feat": dev}, device_id_type=pl.DeviceIdType.MESH)

    def copy_a(idx):
        return remote(zbuf.at[idx, pl.ds((1 - cc) * 128, 128), :], ra.at[idx], as_sem.at[idx], ar_sem.at[idx], sib)

    def copy_b(idx):
        return remote(snd.at[idx], rb.at[idx], bs_sem.at[idx], br_sem.at[idx], far)

    def z_region(idx, first, count):
        if isinstance(idx, int):
            b, j = divmod(idx, 2)
        else:
            b, j = idx // 2, idx % 2
        return rbuf.at[pl.ds(b * HB + first, count), pl.ds(pl.multiple_of(j * 512, 512), 512)]

    def region(idx, first, count):
        if idx >= 4:
            return kx.at[pl.ds((idx - 4) * HB + first, count), pl.ds(0, 512)]
        return z_region(idx, first, count)

    def copy_c(idx):
        r = region(idx, cc * 128 + xx * 64, 64)
        return remote(r, r, cs_sem.at[idx], cr_sem.at[idx], far)

    def copy_d(idx):
        r = region(idx, cc * 128, 128)
        return remote(r, r, ds_sem.at[idx], dr_sem.at[idx], sib)

    def copy_ck(idx):
        r = kv.at[pl.ds((idx - 4) * HB + cc * 128 + xx * 64, 64), :]
        return remote(r, r, ks_sem.at[idx - 4], kr_sem.at[idx - 4], far)

    def copy_dk(idx):
        r = kv.at[pl.ds((idx - 4) * HB + cc * 128, 128), :]
        return remote(r, r, ls_sem.at[idx - 4], lr_sem.at[idx - 4], sib)

    def stage_a(idx):
        copy_a(idx).start()

    def stage_b(idx):
        copy_a(idx).wait_recv()
        o = (1 - xx) * 64
        snd[idx] = zbuf[idx, pl.ds(cc * 128 + o, 64), :] + ra[idx, pl.ds(o, 64), :]
        copy_b(idx).start()

    def stage_c(idx):
        copy_b(idx).wait_recv()
        o = xx * 64
        val = (zbuf[idx, pl.ds(cc * 128 + o, 64), :] + ra[idx, pl.ds(o, 64), :]) + rb[idx]
        if idx < 4:
            j = idx % 2
            res = y_ref[:, j * 512:(j + 1) * 512] - jax.nn.sigmoid(val)
            rbuf[pl.ds((idx // 2) * HB + cc * 128 + o, 64), j * 512:(j + 1) * 512] = res.astype(BF16)
        else:
            if idx == 4:
                for p in range(3):
                    small_g(p).wait_recv()
            nj = ((dall[2 * xx] + dall[2 * xx + 1]) + (dall[2 * (1 - xx)] + dall[2 * (1 - xx) + 1]))[0:1, :]
            first = (idx - 4) * HB + cc * 128 + o
            rid = lax.broadcasted_iota(jnp.int32, (64, N), 0) + first
            cid = lax.broadcasted_iota(jnp.int32, (64, N), 1)
            ni = jnp.sum(jnp.where(rid == cid, nj, 0.0), axis=1, keepdims=True)
            dist = jnp.maximum(ni + nj - 2.0 * val, 0.0)
            kern = jnp.exp(-dist * inv_band)
            kx[pl.ds(first, 64), 0:512] = kern.astype(BF16)
            kv[pl.ds(first, 64), :] = jnp.broadcast_to(jnp.sum(kern, axis=1, keepdims=True), (64, 128))
            copy_ck(idx).start()
        copy_c(idx).start()
        copy_a(idx).wait_send()
        copy_b(idx).wait_send()

    def stage_d(idx):
        copy_c(idx).wait()
        copy_d(idx).start()
        if idx >= 4:
            copy_ck(idx).wait()
            copy_dk(idx).start()

    def stage_e(idx):
        copy_d(idx).wait()
        if idx >= 4:
            copy_dk(idx).wait()

    peers = (sib, far, diag_dev)
    def small_q(p):
        return remote(qall.at[me], qall.at[me], qs_sem.at[p], qr_sem.at[p], peers[p])

    def small_g(p):
        return remote(dall.at[me], dall.at[me], gs_sem.at[p], gr_sem.at[p], peers[p])

    def load_th(b, c):
        v = (pl.ds(b * HB, HB), pl.ds(pl.multiple_of(c * CW, CW), CW))
        return pltpu.make_async_copy(th_hbm.at[v], th.at[v], ld_sem.at[b * NC + c])

    def load_a(j):
        v = (pl.ds(j * 512, 512), slice(None))
        return pltpu.make_async_copy(a_hbm.at[v], a.at[v], a_sem.at[j])

    for c in range(NC):
        load_th(0, c).start()
    for j in range(2):
        load_a(j).start()
    for c in range(NC):
        load_th(1, c).start()

    barrier = pltpu.get_barrier_semaphore()
    for p in peers:
        pl.semaphore_signal(barrier, inc=1, device_id={"feat": p}, device_id_type=pl.DeviceIdType.MESH)
    pl.semaphore_wait(barrier, 3)

    def out_theta():
        return pltpu.make_async_copy(th, th_out, out_sem.at[0])

    def out_s(b):
        v = (pl.ds(b * HB, HB), slice(None))
        return pltpu.make_async_copy(sbuf.at[v], s_out.at[v], out_sem.at[1 + b])

    def step(s, carry):
        par = s % 2
        old = 1 - par
        new_rows = (512 * par, HB)
        obase = 256 * old

        def project(b, c0, xb):
            part = lax.dot_general(ut_ref[:, c0], xb, NT, preferred_element_type=F32)
            qacc[:, b * HB:(b + 1) * HB] += part

        def load_phase(b):
            def body(c, carry):
                load_th(b, c).wait()
                for i in range(CW // SW):
                    cs = pl.ds(pl.multiple_of(c * CW + i * SW, SW), SW)
                    t = th[b * HB:(b + 1) * HB, cs]
                    tb[pl.ds(pl.multiple_of(new_rows[b], HB), HB), cs] = t.astype(BF16)
                    project(b, cs, (t - mu_ref[:, cs]).astype(BF16))
                return carry
            lax.fori_loop(0, NC, body, 0)

        def update_phase(b):
            def body(c, carry):
                if b == 1:
                    k_events(c)
                kb = kx[b * HB:(b + 1) * HB, 0:512]
                kt = kx[b * HB:(b + 1) * HB, pl.ds(pl.multiple_of(obase, HB), 512)]
                kvb = kv[b * HB:(b + 1) * HB, 0:1]
                for i in range(CW // SW):
                    cs = pl.ds(pl.multiple_of(c * CW + i * SW, SW), SW)
                    drive = jnp.dot(kb, sbuf[:, cs], preferred_element_type=F32)
                    pull = jnp.dot(kt, tb[pl.ds(pl.multiple_of(obase, HB), 512), cs], preferred_element_type=F32)
                    t = th[b * HB:(b + 1) * HB, cs]
                    t = t + gain * (drive + two_over_band * (kvb * t - pull))
                    th[b * HB:(b + 1) * HB, cs] = t
                    tb[pl.ds(pl.multiple_of(new_rows[b], HB), HB), cs] = t.astype(BF16)
                    project(b, cs, (t - mu_ref[:, cs]).astype(BF16))
                return carry
            lax.fori_loop(0, NC, body, 0)

        def k_events(c):
            @pl.when(c == 0)
            def _():
                stage_b(0)

            @pl.when(c == 1)
            def _():
                stage_b(1)

            @pl.when(c == 2)
            def _():
                stage_c(0)

            @pl.when(c == 3)
            def _():
                stage_c(1)

        qacc[...] = jnp.zeros_like(qacc)
        for b in range(2):
            @pl.when(s == 0)
            def _():
                load_phase(b)
                if b == 1:
                    stage_b(0)
                    stage_b(1)
                    stage_c(0)
                    stage_c(1)

            @pl.when(s > 0)
            def _():
                update_phase(b)

            if b == 1:
                qall[me] = qacc[...]
                for p in range(3):
                    small_q(p).start()

                @pl.when(s == NUM_STEPS - 1)
                def _():
                    out_theta().start()

            def logits(j, carry):
                @pl.when(s == 0)
                def _():
                    if b == 0:
                        load_a(j).wait()
                idx = 2 * b + j
                if b == 1:
                    @pl.when(j == 0)
                    def _():
                        stage_d(0)

                    @pl.when(j == 1)
                    def _():
                        stage_d(1)
                zbuf[idx] = lax.dot_general(
                    tb[pl.ds(pl.multiple_of(new_rows[b], HB), HB), :],
                    a[pl.ds(pl.multiple_of(j * 512, 512), 512), :], NT, preferred_element_type=F32)
                stage_a(idx)
                return carry
            lax.fori_loop(0, 2, logits, 0)

        stage_b(2)
        nbase = 256 * par

        def gram(b, carry):
            rows = jnp.where(b == 0, 512 * par, HB)
            g = lax.dot_general(
                tb[pl.ds(pl.multiple_of(rows, HB), HB), :],
                tb[pl.ds(pl.multiple_of(nbase, HB), 512), :], NT, preferred_element_type=F32)
            zbuf[4 + b, :, pl.ds(pl.multiple_of(nbase, HB), HB)] = g[:, 0:HB]
            zbuf[4 + b, :, pl.ds(pl.multiple_of(HB - nbase, HB), HB)] = g[:, HB:]
            own = zbuf[4 + b, :, pl.ds(pl.multiple_of(b * HB, HB), HB)]
            eye = lax.broadcasted_iota(jnp.int32, (HB, HB), 0) == lax.broadcasted_iota(jnp.int32, (HB, HB), 1)
            row = jnp.sum(jnp.where(eye, own, 0.0), axis=0, keepdims=True)
            dgs[:, pl.ds(pl.multiple_of(b * HB, HB), HB)] = jnp.broadcast_to(row, (8, HB))
            stage_a(4 + b)

            @pl.when(b == 0)
            def _():
                stage_b(3)
            return carry
        lax.fori_loop(0, 2, gram, 0)
        dall[me] = dgs[...]
        for p in range(3):
            small_g(p).start()
        stage_b(4)
        stage_c(2)
        stage_e(0)
        stage_e(1)
        for p in range(3):
            small_q(p).wait_recv()
        qsum = (qall[0] + qall[1]) + (qall[2] + qall[3])
        qt[...] = jnp.concatenate([qsum, jnp.zeros((112, N), F32)], axis=0).T

        def score_phase(b):
            def body(c, carry):
                events = {(0, 1): ((stage_b, 5), (stage_c, 3), (stage_d, 2)),
                          (0, 2): ((stage_c, 4), (stage_d, 3)),
                          (0, 3): ((stage_c, 5),),
                          (1, 0): ((stage_d, 4),),
                          (1, 1): ((stage_d, 5),)}
                for (eb, ec), todo in events.items():
                    if eb == b:
                        @pl.when(c == ec)
                        def _():
                            for f, i in todo:
                                f(i)
                rr = rbuf[b * HB:(b + 1) * HB, :]
                qb = qt[b * HB:(b + 1) * HB, 0:16].astype(BF16)
                for i in range(CW // SW):
                    cs = pl.ds(pl.multiple_of(c * CW + i * SW, SW), SW)
                    lik = jnp.dot(rr, a[:, cs], preferred_element_type=F32)
                    low = jnp.dot(qb, ut_ref[:, cs], preferred_element_type=F32)
                    x = th[b * HB:(b + 1) * HB, cs] - mu_ref[:, cs]
                    sbuf[b * HB:(b + 1) * HB, cs] = (lik_weight * lik - x * lam_ref[:, cs] - low).astype(BF16)
                return carry
            lax.fori_loop(0, NC, body, 0)

        for b in range(2):
            if b == 1:
                stage_e(2)
                stage_e(3)
            score_phase(b)

            @pl.when(s == NUM_STEPS - 1)
            def _():
                out_s(b).start()
        stage_e(4)
        stage_e(5)
        for p in range(3):
            small_q(p).wait_send()
            small_g(p).wait_send()
        kx[:, 512:768] = kx[:, 0:256]
        return carry

    lax.fori_loop(0, NUM_STEPS, step, 0)
    k_copy = pltpu.make_async_copy(kx.at[:, pl.ds(0, 512)], k_out, out_sem.at[3])
    kv_copy = pltpu.make_async_copy(kv, kv_out, out_sem.at[4])
    k_copy.start()
    kv_copy.start()
    k_copy.wait()
    kv_copy.wait()
    out_theta().wait()
    out_s(0).wait()
    out_s(1).wait()


def last_kernel(consts, kb, kv, s, th, out):
    _, _, two_over_band, gain = consts
    for i in range(2):
        r = slice(i * HB, (i + 1) * HB)
        k = kb[r, :]
        t = th[...]
        drive = jnp.dot(k, s[...], preferred_element_type=F32)
        pull = jnp.dot(k, t.astype(BF16), preferred_element_type=F32)
        t = th[r, :]
        out[r, :] = t + gain * (drive + two_over_band * (kv[r, 0:1] * t - pull))


def solution(mesh):
    feat = mesh.shape["feat"]
    dim_full = D * feat
    band = 2.0 * dim_full
    consts = (2.0 / math.sqrt(M * dim_full), 1.0 / band, 2.0 / band, dim_full / 4.0 / N)

    def local_run(particles, prec_diag, low_factor, prior_mean, data_mat, labels):
        targets = labels.astype(F32)[None, :]
        vm = pl.BlockSpec(memory_space=pltpu.VMEM)
        anyspace = pl.BlockSpec(memory_space=pl.ANY)
        dma = pltpu.SemaphoreType.DMA
        th2, s2, k2, kv2 = pl.pallas_call(
            functools.partial(run_kernel, consts),
            out_shape=(jax.ShapeDtypeStruct((N, D), F32), jax.ShapeDtypeStruct((N, D), BF16),
                       jax.ShapeDtypeStruct((N, N), BF16), jax.ShapeDtypeStruct((N, 128), F32)),
            in_specs=[anyspace, vm, vm, vm, anyspace, vm],
            out_specs=(anyspace,) * 4,
            scratch_shapes=[
                pltpu.VMEM((N, D), F32), pltpu.VMEM((M, D), BF16), pltpu.VMEM((768, D), BF16),
                pltpu.VMEM((N, D), BF16),
                pltpu.VMEM((6, HB, 512), F32), pltpu.VMEM((6, 128, 512), F32), pltpu.VMEM((6, 64, 512), F32),
                pltpu.VMEM((6, 64, 512), F32), pltpu.VMEM((N, M), BF16), pltpu.VMEM((N, 768), BF16),
                pltpu.VMEM((N, 128), F32), pltpu.VMEM((16, N), F32), pltpu.VMEM((4, 16, N), F32),
                pltpu.VMEM((8, N), F32), pltpu.VMEM((4, 8, N), F32), pltpu.VMEM((N, 128), F32),
                dma((8,)), dma((2,)), dma((5,)),
                dma((6,)), dma((6,)), dma((6,)), dma((6,)), dma((6,)), dma((6,)), dma((6,)), dma((6,)),
                dma((2,)), dma((2,)), dma((2,)), dma((2,)),
                dma((3,)), dma((3,)), dma((3,)), dma((3,)),
            ],
            compiler_params=pltpu.CompilerParams(
                collective_id=0, has_side_effects=True, vmem_limit_bytes=VMEM_LIMIT),
        )(particles, prec_diag[None, :], low_factor.T, prior_mean[None, :], data_mat, targets)
        width = 1024
        return pl.pallas_call(
            functools.partial(last_kernel, consts),
            grid=(D // width,),
            out_shape=jax.ShapeDtypeStruct((N, D), F32),
            in_specs=[pl.BlockSpec((N, N), lambda i: (0, 0)), pl.BlockSpec((N, 128), lambda i: (0, 0)),
                      pl.BlockSpec((N, width), lambda i: (0, i)), pl.BlockSpec((N, width), lambda i: (0, i))],
            out_specs=pl.BlockSpec((N, width), lambda i: (0, i)),
            compiler_params=pltpu.CompilerParams(vmem_limit_bytes=48 * 2**20),
        )(k2, kv2, s2, th2)

    return jax.shard_map(
        local_run,
        mesh=mesh,
        in_specs=(P("ens", "feat"), P(("ens", "feat")), P(("ens", "feat"), None),
                  P(("ens", "feat")), P("ens", "feat"), P("ens")),
        out_specs=P("ens", "feat"),
        check_vma=False,
    )
```

time: 537 us -> 197 us (0.37); the launches traced: 529 us -> 197 us
  matrix products: 329 us -> 0 us
  Pallas kernels: 0 us -> 193 us
  waiting for transfers between devices: 93.5 us -> 0 us
  blocking collectives: 61.4 us -> 0 us
  local copies, waits for them, and re-layouts: 26 us -> 1.98 us
  between operations: 13.7 us -> 0.02 us
    dot_general x18 -> x0, matrix products: 329 us -> none  [the longest x3 89.8 us: local_run(): pulled = jnp.dot(kern_bf, part_bf, preferred_element_type=jnp.float32)]
    pallas_call x0 -> x2, Pallas kernels: none -> 193 us  [the longest x1 173 us: local_run(): pl.pallas_call(functools.partial(run_kernel, consts), out_shape=(jax.Shap...]
    psum x3 -> x0, waiting for transfers between devices: 93.4 us -> none  [local_run(): lax.psum(lax.dot_general(part_bf, data_mat, DIMS_NT, preferred_element_ty...]
    psum x3 -> x0, blocking collectives: 61.4 us -> none  [local_run(): lax.psum(jnp.dot(centred.astype(jnp.bfloat16), low_factor, preferred_elem...]
    gather x3 -> x0, local copies, waits for them, and re-layouts: 26 us -> none  [local_run(): sq_norm = jnp.diagonal(gram_mat)]
  transfers between devices with their start and end apart: 3 -> 0, of which waited for: 3 -> 0; matrix products, arithmetic and copies ran while one was open for 9% -> 0% of each run, Pallas kernels for 0% -> 0%
where the time goes in v1:
time: 197 us
  Pallas kernels  193 us (98%)
  local copies, waits for them, and re-layouts  1.98 us (1%)
    pallas_call x1, Pallas kernels, local_run(): pl.pallas_call(functools.partial(run_kernel, consts), out_shape=(jax.Shap...  173 us
    pallas_call x1, Pallas kernels, local_run(): pl.pallas_call(functools.partial(last_kernel, consts), grid=(D // width,)...  20.4 us

profile of v1, /device:TPU:0, one launch (start us, length us, event | category | flops | bytes accessed | tf_op | source)
XLA Modules:
  0.0 196.7 jit_solution(6622182534362322444)
XLA Ops:
  0.0 1.3 convert_element_type.3
  1.3 173.1 %shard_map.64 = (f32[512,8192]{1,0:T(8,128)}, bf16[512,8192]{1,0:T(8,128)(2,1)}, bf16[512,512]{1,0:T(8,128)(2,1)}, f32[512,128]{1,0:T(8,128)}) custom-call(f32[512,8192]{1,0:T(8,128)} %th_hbm.1, f32[1,8192]{1,0:T(1,128)} %bitcast.5, bf16[16,8192]{1,0:T(8,128)(2,1)} %bitcast.4, f32[1,8192]{1,0:T(1,128)} %bitcast.6, bf16[1024,8192]{1,0:T(8,128)(2,1)} %a_hbm.1, ...), custom_call_target="tpu_custom_call" | custom-call | tf_op jit(solution)/shard_map/pallas_call | solution.py:371
  174.3 0.0 copy-start
  174.4 1.0 copy-done
  175.4 0.0 copy-start.1
  175.4 0.9 copy-done.1
  176.3 20.4 %shard_map.65 = f32[512,8192]{1,0:T(8,128)} custom-call(bf16[512,512]{1,0:T(8,128)(2,1)S(1)} %copy-done, f32[512,128]{1,0:T(8,128)S(1)} %copy-done.1, bf16[512,8192]{1,0:T(8,128)(2,1)} %get-tuple-element.11.s, f32[512,8192]{1,0:T(8,128)} %get-tuple-element.12.th), custom_call_target="tpu_custom_call" | custom-call | tf_op jit(solution)/shard_map/pallas_call | solution.py:393
Async XLA Ops:
  174.3 1.0 copy-start
  175.4 0.9 copy-start.1

commit v2 on v1

v2 whole, which is shorter than its diff:
```python
import functools
import math
import jax
import jax.numpy as jnp
from jax import lax
from jax.experimental import pallas as pl
from jax.experimental.pallas import tpu as pltpu
from jax.sharding import PartitionSpec as P

NUM_STEPS = 3
NT = (((1,), (1,)), ((), ()))
F32 = jnp.float32
BF16 = jnp.bfloat16
N = 512
HB = 256
D = 8192
M = 1024
CW = 2048
SW = 1024
SS = 512
NC = D // CW
VMEM_LIMIT = 67_043_328


def run_kernel(consts, th_hbm, lam_ref, ut_ref, mu_ref, a_hbm, y_ref,
               th_out, s_out, k_out, kv_out,
               th, a, tb, tn, sbuf, zbuf, ra, snd, rb, rbuf, kx, kv, qacc, qall, dall, kall, qt,
               ld_sem, a_sem, out_sem, tn_sem, as_sem, ar_sem, bs_sem, br_sem, cs_sem, cr_sem, ds_sem, dr_sem,
               qs_sem, qr_sem, gs_sem, gr_sem, ks_sem, kr_sem):
    lik_weight, inv_band, two_over_band, gain = consts
    me = lax.axis_index("feat")
    xx = me // 2
    cc = me % 2
    sib = xx * 2 + (1 - cc)
    far = (1 - xx) * 2 + cc
    diag_dev = (1 - xx) * 2 + (1 - cc)
    peers = (sib, far, diag_dev)

    def remote(src, dst, ssem, rsem, dev):
        return pltpu.make_async_remote_copy(
            src_ref=src, dst_ref=dst, send_sem=ssem, recv_sem=rsem,
            device_id={"feat": dev}, device_id_type=pl.DeviceIdType.MESH)

    def width(idx):
        return 256 if idx == 4 else 512

    def block(idx):
        return idx // 2 if idx < 4 else idx - 4

    def copy_a(idx):
        w = pl.ds(0, width(idx))
        return remote(zbuf.at[idx, pl.ds((1 - cc) * 128, 128), w], ra.at[idx, :, w],
                      as_sem.at[idx], ar_sem.at[idx], sib)

    def copy_b(idx):
        w = pl.ds(0, width(idx))
        return remote(snd.at[idx, :, w], rb.at[idx, :, w], bs_sem.at[idx], br_sem.at[idx], far)

    def region(idx, first, count):
        rows = pl.ds(block(idx) * HB + first, count)
        if idx >= 4:
            return kx.at[rows, pl.ds(0, width(idx))]
        return rbuf.at[rows, pl.ds((idx % 2) * 512, 512)]

    def copy_c(idx):
        r = region(idx, cc * 128 + xx * 64, 64)
        return remote(r, r, cs_sem.at[idx], cr_sem.at[idx], far)

    def copy_d(idx):
        r = region(idx, cc * 128, 128)
        return remote(r, r, ds_sem.at[idx], dr_sem.at[idx], sib)

    def small(buf, ssem, rsem, p):
        return remote(buf.at[me], buf.at[me], ssem.at[p], rsem.at[p], peers[p])

    small_q = functools.partial(small, qall, qs_sem, qr_sem)
    small_g = functools.partial(small, dall, gs_sem, gr_sem)
    small_k = functools.partial(small, kall, ks_sem, kr_sem)

    def stage_a(idx):
        copy_a(idx).start()

    def stage_b(idx):
        copy_a(idx).wait_recv()
        o = (1 - xx) * 64
        w = width(idx)
        snd[idx, :, 0:w] = zbuf[idx, pl.ds(cc * 128 + o, 64), 0:w] + ra[idx, pl.ds(o, 64), 0:w]
        copy_b(idx).start()

    def stage_c(idx):
        copy_b(idx).wait_recv()
        o = xx * 64
        w = width(idx)
        val = (zbuf[idx, pl.ds(cc * 128 + o, 64), 0:w] + ra[idx, pl.ds(o, 64), 0:w]) + rb[idx, :, 0:w]
        first = block(idx) * HB + cc * 128 + o
        if idx < 4:
            j = idx % 2
            res = y_ref[:, j * 512:(j + 1) * 512].astype(F32) - jax.nn.sigmoid(val)
            rbuf[pl.ds(first, 64), j * 512:(j + 1) * 512] = res.astype(BF16)
        else:
            if idx == 4:
                for p in range(3):
                    small_g(p).wait_recv()
            nj = ((dall[2 * xx] + dall[2 * xx + 1]) + (dall[2 * (1 - xx)] + dall[2 * (1 - xx) + 1]))[0:1, :]
            rid = lax.broadcasted_iota(jnp.int32, (64, N), 0) + first
            cid = lax.broadcasted_iota(jnp.int32, (64, N), 1)
            ni = jnp.sum(jnp.where(rid == cid, nj, 0.0), axis=1, keepdims=True)
            dist = jnp.maximum(ni + nj[:, 0:w] - 2.0 * val, 0.0)
            kern = jnp.exp(-dist * inv_band)
            kx[pl.ds(first, 64), 0:w] = kern.astype(BF16)
            col = jnp.sum(kern, axis=0, keepdims=True)
            if idx == 4:
                kall[me, :, 0:HB] = jnp.broadcast_to(col, (8, HB))
            else:
                kall[me, :, 0:HB] += jnp.broadcast_to(col[:, 0:HB], (8, HB))
                cross = jnp.sum(kern[:, 0:HB], axis=1, keepdims=True)
                placed = jnp.sum(jnp.where(rid[:, HB:] == cid[:, HB:], cross, 0.0), axis=0, keepdims=True)
                kall[me, :, HB:N] = jnp.broadcast_to(col[:, HB:N] + placed, (8, HB))
                for p in range(3):
                    small_k(p).start()
        copy_c(idx).start()
        copy_a(idx).wait_send()
        copy_b(idx).wait_send()

    def stage_d(idx):
        copy_c(idx).wait()
        copy_d(idx).start()

    def stage_e(idx):
        copy_d(idx).wait()

    def load_th(b, c):
        v = (pl.ds(b * HB, HB), pl.ds(pl.multiple_of(c * CW, CW), CW))
        return pltpu.make_async_copy(th_hbm.at[v], th.at[v], ld_sem.at[b * NC + c])

    def load_a(j):
        v = (pl.ds(j * 512, 512), slice(None))
        return pltpu.make_async_copy(a_hbm.at[v], a.at[v], a_sem.at[j])

    for c in range(NC):
        load_th(0, c).start()
    for j in range(2):
        load_a(j).start()
    for c in range(NC):
        load_th(1, c).start()

    barrier = pltpu.get_barrier_semaphore()
    for p in peers:
        pl.semaphore_signal(barrier, inc=1, device_id={"feat": p}, device_id_type=pl.DeviceIdType.MESH)
    pl.semaphore_wait(barrier, 3)

    def out_theta():
        return pltpu.make_async_copy(th, th_out, out_sem.at[0])

    def out_s(b):
        v = (pl.ds(b * HB, HB), slice(None))
        return pltpu.make_async_copy(sbuf.at[v], s_out.at[v], out_sem.at[1 + b])

    def keep_block0():
        return pltpu.make_async_copy(tn, tb.at[pl.ds(0, HB), :], tn_sem.at[0])

    def new_block(b):
        return tn if b == 0 else tb.at[pl.ds(HB, HB), :]

    def step(s, carry):
        def at(cond, *todo):
            @pl.when(cond)
            def _():
                for f, i in todo:
                    f(i)

        def project(b, cs, xb):
            part = lax.dot_general(ut_ref[:, cs], xb, NT, preferred_element_type=F32)
            qacc[:, b * HB:(b + 1) * HB] += part

        def load_phase(b):
            def body(c, carry):
                load_th(b, c).wait()
                for i in range(CW // SW):
                    cs = pl.ds(pl.multiple_of(c * CW + i * SW, SW), SW)
                    t = th[b * HB:(b + 1) * HB, cs]
                    new_block(b)[:, cs] = t.astype(BF16)
                    project(b, cs, (t - mu_ref[:, cs]).astype(BF16))
                return carry
            lax.fori_loop(0, NC, body, 0)

        def update_phase(b):
            def body(c, carry):
                if b == 1:
                    at(c == 1, (stage_b, 4))
                    at(c == 2, (stage_c, 0))
                kb = kx[b * HB:(b + 1) * HB, 0:N]
                kt = kx[b * HB:(b + 1) * HB, N:2 * N]
                kvb = kv[b * HB:(b + 1) * HB, 0:1]
                for i in range(CW // SW):
                    cs = pl.ds(pl.multiple_of(c * CW + i * SW, SW), SW)
                    move = (jnp.dot(kb, sbuf[:, cs], preferred_element_type=F32)
                            + jnp.dot(kt, tb[:, cs], preferred_element_type=F32))
                    t = th[b * HB:(b + 1) * HB, cs]
                    t = t + gain * (move + kvb * t)
                    th[b * HB:(b + 1) * HB, cs] = t
                    new_block(b)[:, cs] = t.astype(BF16)
                    project(b, cs, (t - mu_ref[:, cs]).astype(BF16))
                return carry
            lax.fori_loop(0, NC, body, 0)

        def logits(b, j):
            zbuf[2 * b + j] = lax.dot_general(
                new_block(b)[...], a[j * 512:(j + 1) * 512, :], NT, preferred_element_type=F32)
            stage_a(2 * b + j)

        def gram(b, cols):
            g = lax.dot_general(new_block(b)[...], new_block(cols)[...], NT, preferred_element_type=F32)
            zbuf[4 + b, :, cols * HB:(cols + 1) * HB] = g
            if cols == b:
                eye = lax.broadcasted_iota(jnp.int32, (HB, HB), 0) == lax.broadcasted_iota(jnp.int32, (HB, HB), 1)
                row = jnp.sum(jnp.where(eye, g, 0.0), axis=0, keepdims=True)
                dall[me, :, b * HB:(b + 1) * HB] = jnp.broadcast_to(row, (8, HB))

        def first_gram():
            gram(0, 0)
            stage_a(4)
            stage_b(1)

        qacc[...] = jnp.zeros_like(qacc)

        @pl.when(s == 0)
        def _():
            load_phase(0)
            load_a(0).wait()

        @pl.when(s > 0)
        def _():
            update_phase(0)

        logits(0, 0)

        @pl.when(s == 0)
        def _():
            load_a(1).wait()
        logits(0, 1)
        stage_b(0)

        @pl.when(s == 0)
        def _():
            first_gram()
            load_phase(1)
            stage_b(4)

        @pl.when(s > 0)
        def _():
            first_gram()
            update_phase(1)
            stage_c(1)

        qall[me] = qacc[...]
        for p in range(3):
            small_q(p).start()

        @pl.when(s == NUM_STEPS - 1)
        def _():
            out_theta().start()

        @pl.when(s < NUM_STEPS - 1)
        def _():
            keep_block0().start()

        logits(1, 0)
        at(s == 0, (stage_c, 0))
        at(s > 0, (stage_d, 0))
        logits(1, 1)
        at(s == 0, (stage_c, 1))
        at(s > 0, (stage_d, 1))
        stage_b(2)
        gram(1, 0)
        at(s == 0, (stage_d, 0))
        gram(1, 1)
        stage_a(5)
        for p in range(3):
            small_g(p).start()
        stage_b(3)
        at(s == 0, (stage_d, 1))
        stage_e(0)
        stage_e(1)
        for p in range(3):
            small_q(p).wait_recv()
        qsum = (qall[0] + qall[1]) + (qall[2] + qall[3])
        qt[...] = jnp.concatenate([qsum, jnp.zeros((112, N), F32)], axis=0).T

        def score_phase(b, events):
            def body(c, carry):
                for when, todo in events.items():
                    at(c == when, *todo)
                rr = rbuf[b * HB:(b + 1) * HB, :]
                qb = qt[b * HB:(b + 1) * HB, 0:16].astype(BF16)
                for i in range(CW // SS):
                    cs = pl.ds(pl.multiple_of(c * CW + i * SS, SS), SS)
                    lik = jnp.dot(rr, a[:, cs], preferred_element_type=F32)
                    low = jnp.dot(qb, ut_ref[:, cs], preferred_element_type=F32)
                    x = th[b * HB:(b + 1) * HB, cs] - mu_ref[:, cs]
                    sbuf[b * HB:(b + 1) * HB, cs] = (lik_weight * lik - x * lam_ref[:, cs] - low).astype(BF16)
                return carry
            lax.fori_loop(0, NC, body, 0)

            @pl.when(s == NUM_STEPS - 1)
            def _():
                out_s(b).start()

        score_phase(0, {1: [(stage_c, 2)], 2: [(stage_c, 4)], 3: [(stage_c, 3), (stage_b, 5)]})
        for idx in (2, 3, 4):
            stage_d(idx)
        stage_e(2)
        stage_e(3)
        score_phase(1, {2: [(stage_c, 5)]})
        stage_e(4)
        stage_d(5)
        for p in range(3):
            small_k(p).wait_recv()
        ksum = (kall[0] + kall[1]) + (kall[2] + kall[3])
        kv[...] = jnp.broadcast_to(two_over_band * ksum[0:1, :], (128, N)).T
        stage_e(5)
        kx[0:HB, HB:N] = kx[HB:N, 0:HB].astype(F32).T.astype(BF16)
        kx[:, N:2 * N] = (kx[:, 0:N].astype(F32) * -two_over_band).astype(BF16)
        for p in range(3):
            small_q(p).wait_send()
            small_g(p).wait_send()
            small_k(p).wait_send()

        @pl.when(s < NUM_STEPS - 1)
        def _():
            keep_block0().wait()
        return carry

    lax.fori_loop(0, NUM_STEPS, step, 0)
    k_copy = pltpu.make_async_copy(kx, k_out, out_sem.at[3])
    kv_copy = pltpu.make_async_copy(kv, kv_out, out_sem.at[4])
    k_copy.start()
    kv_copy.start()
    k_copy.wait()
    kv_copy.wait()
    out_theta().wait()
    out_s(0).wait()
    out_s(1).wait()


def last_kernel(gain, kx, kv, s, th, out):
    for i in range(s.shape[1] // 512):
        cs = slice(i * 512, (i + 1) * 512)
        t = th[:, cs]
        move = (jnp.dot(kx[:, 0:N], s[:, cs], preferred_element_type=F32)
                + jnp.dot(kx[:, N:2 * N], t.astype(BF16), preferred_element_type=F32))
        out[:, cs] = t + gain * (move + kv[:, 0:1] * t)


def solution(mesh):
    feat = mesh.shape["feat"]
    dim_full = D * feat
    band = 2.0 * dim_full
    consts = (2.0 / math.sqrt(M * dim_full), 1.0 / band, 2.0 / band, dim_full / 4.0 / N)

    def local_run(particles, prec_diag, low_factor, prior_mean, data_mat, labels):
        targets = labels[None, :]
        vm = pl.BlockSpec(memory_space=pltpu.VMEM)
        anyspace = pl.BlockSpec(memory_space=pl.ANY)
        dma = pltpu.SemaphoreType.DMA
        th2, s2, k2, kv2 = pl.pallas_call(
            functools.partial(run_kernel, consts),
            out_shape=(jax.ShapeDtypeStruct((N, D), F32), jax.ShapeDtypeStruct((N, D), BF16),
                       jax.ShapeDtypeStruct((N, 2 * N), BF16), jax.ShapeDtypeStruct((N, 128), F32)),
            in_specs=[anyspace, vm, vm, vm, anyspace, vm],
            out_specs=(anyspace,) * 4,
            scratch_shapes=[
                pltpu.VMEM((N, D), F32), pltpu.VMEM((M, D), BF16), pltpu.VMEM((N, D), BF16), pltpu.VMEM((HB, D), BF16),
                pltpu.VMEM((N, D), BF16),
                pltpu.VMEM((6, HB, 512), F32), pltpu.VMEM((6, 128, 512), F32), pltpu.VMEM((6, 64, 512), F32),
                pltpu.VMEM((6, 64, 512), F32), pltpu.VMEM((N, M), BF16), pltpu.VMEM((N, 2 * N), BF16),
                pltpu.VMEM((N, 128), F32), pltpu.VMEM((16, N), F32), pltpu.VMEM((4, 16, N), F32),
                pltpu.VMEM((4, 8, N), F32), pltpu.VMEM((4, 8, N), F32), pltpu.VMEM((N, 128), F32),
                dma((8,)), dma((2,)), dma((5,)), dma((1,)),
                dma((6,)), dma((6,)), dma((6,)), dma((6,)), dma((6,)), dma((6,)), dma((6,)), dma((6,)),
                dma((3,)), dma((3,)), dma((3,)), dma((3,)), dma((3,)), dma((3,)),
            ],
            compiler_params=pltpu.CompilerParams(
                collective_id=0, has_side_effects=True, vmem_limit_bytes=VMEM_LIMIT),
        )(particles, prec_diag[None, :], low_factor.T, prior_mean[None, :], data_mat, targets)
        width = 1024
        return pl.pallas_call(
            functools.partial(last_kernel, consts[3]),
            grid=(D // width,),
            out_shape=jax.ShapeDtypeStruct((N, D), F32),
            in_specs=[pl.BlockSpec((N, 2 * N), lambda i: (0, 0)), pl.BlockSpec((N, 128), lambda i: (0, 0)),
                      pl.BlockSpec((N, width), lambda i: (0, i)), pl.BlockSpec((N, width), lambda i: (0, i))],
            out_specs=pl.BlockSpec((N, width), lambda i: (0, i)),
            compiler_params=pltpu.CompilerParams(vmem_limit_bytes=VMEM_LIMIT),
        )(k2, kv2, s2, th2)

    return jax.shard_map(
        local_run,
        mesh=mesh,
        in_specs=(P("ens", "feat"), P(("ens", "feat")), P(("ens", "feat"), None),
                  P(("ens", "feat")), P("ens", "feat"), P("ens")),
        out_specs=P("ens", "feat"),
        check_vma=False,
    )
```

time: 197 us -> 174 us (0.88)
  Pallas kernels: 193 us -> 174 us
  local copies, waits for them, and re-layouts: 1.98 us -> 0 us
    pallas_call x1, Pallas kernels: 173 us -> 153 us  [local_run(): pl.pallas_call(functools.partial(run_kernel, consts), out_shape=(jax.Shap...]
    unnamed x4 -> x0, local copies, waits for them, and re-layouts: 1.98 us -> none
where the time goes in v2:
time: 174 us
  Pallas kernels  174 us (100%)
    pallas_call x1, Pallas kernels, local_run(): pl.pallas_call(functools.partial(run_kernel, consts), out_shape=(jax.Shap...  153 us
    pallas_call x1, Pallas kernels, local_run(): pl.pallas_call(functools.partial(last_kernel, consts[3]), grid=(D // widt...  20.6 us

profile of v2, /device:TPU:0, one launch (start us, length us, event | category | flops | bytes accessed | tf_op | source)
XLA Modules:
  0.0 173.8 jit_solution(14044270610040995791)
XLA Ops:
  0.0 153.2 %shard_map.64 = (f32[512,8192]{1,0:T(8,128)}, bf16[512,8192]{1,0:T(8,128)(2,1)}, bf16[512,1024]{1,0:T(8,128)(2,1)}, f32[512,128]{1,0:T(8,128)}) custom-call(f32[512,8192]{1,0:T(8,128)} %th_hbm.1, f32[1,8192]{1,0:T(1,128)} %bitcast.5, bf16[16,8192]{1,0:T(8,128)(2,1)} %bitcast.4, f32[1,8192]{1,0:T(1,128)} %bitcast.6, bf16[1024,8192]{1,0:T(8,128)(2,1)} %a_hbm.1, ...), custom_call_target="tpu_custom_call" | custom-call | tf_op jit(solution)/shard_map/pallas_call | solution.py:366
  153.2 20.6 %shard_map.65 = f32[512,8192]{1,0:T(8,128)} custom-call(bf16[512,1024]{1,0:T(8,128)(2,1)} %get-tuple-element.9.kx, f32[512,128]{1,0:T(8,128)} %get-tuple-element.10.kv, bf16[512,8192]{1,0:T(8,128)(2,1)} %get-tuple-element.11.s, f32[512,8192]{1,0:T(8,128)} %get-tuple-element.12.th), custom_call_target="tpu_custom_call" | custom-call | tf_op jit(solution)/shard_map/pallas_call | solution.py:387

commit v3 on v2

--- a/solution.py
+++ b/solution.py
@@ -19,6 +19,8 @@
 SW = 1024
 SS = 512
 NC = D // CW
+LW = 1024
+AHEAD = 4
 VMEM_LIMIT = 67_043_328
 
 
@@ -98,7 +100,7 @@
             res = y_ref[:, j * 512:(j + 1) * 512].astype(F32) - jax.nn.sigmoid(val)
             rbuf[pl.ds(first, 64), j * 512:(j + 1) * 512] = res.astype(BF16)
         else:
-            if idx == 4:
+            if idx == 5:
                 for p in range(3):
                     small_g(p).wait_recv()
             nj = ((dall[2 * xx] + dall[2 * xx + 1]) + (dall[2 * (1 - xx)] + dall[2 * (1 - xx) + 1]))[0:1, :]
@@ -110,14 +112,14 @@
             kx[pl.ds(first, 64), 0:w] = kern.astype(BF16)
             col = jnp.sum(kern, axis=0, keepdims=True)
             if idx == 4:
-                kall[me, :, 0:HB] = jnp.broadcast_to(col, (8, HB))
+                kall[me, :, 0:HB] += jnp.broadcast_to(col, (8, HB))
+                for p in range(3):
+                    small_k(p).start()
             else:
-                kall[me, :, 0:HB] += jnp.broadcast_to(col[:, 0:HB], (8, HB))
+                kall[me, :, 0:HB] = jnp.broadcast_to(col[:, 0:HB], (8, HB))
                 cross = jnp.sum(kern[:, 0:HB], axis=1, keepdims=True)
                 placed = jnp.sum(jnp.where(rid[:, HB:] == cid[:, HB:], cross, 0.0), axis=0, keepdims=True)
                 kall[me, :, HB:N] = jnp.broadcast_to(col[:, HB:N] + placed, (8, HB))
-                for p in range(3):
-                    small_k(p).start()
         copy_c(idx).start()
         copy_a(idx).wait_send()
         copy_b(idx).wait_send()
@@ -133,16 +135,12 @@
         v = (pl.ds(b * HB, HB), pl.ds(pl.multiple_of(c * CW, CW), CW))
         return pltpu.make_async_copy(th_hbm.at[v], th.at[v], ld_sem.at[b * NC + c])
 
-    def load_a(j):
-        v = (pl.ds(j * 512, 512), slice(None))
-        return pltpu.make_async_copy(a_hbm.at[v], a.at[v], a_sem.at[j])
+    def load_a(j, c):
+        v = (pl.ds(j * 512 + c * 128, 128), slice(None))
+        return pltpu.make_async_copy(a_hbm.at[v], a.at[v], a_sem.at[j * 4 + c])
 
     for c in range(NC):
         load_th(0, c).start()
-    for j in range(2):
-        load_a(j).start()
-    for c in range(NC):
-        load_th(1, c).start()
 
     barrier = pltpu.get_barrier_semaphore()
     for p in peers:
@@ -169,26 +167,33 @@
                 for f, i in todo:
                     f(i)
 
-        def project(b, cs, xb):
-            part = lax.dot_general(ut_ref[:, cs], xb, NT, preferred_element_type=F32)
-            qacc[:, b * HB:(b + 1) * HB] += part
+        def project():
+            def body(c, carry):
+                at(c == 2, (stage_b, 3))
+                cs = pl.ds(pl.multiple_of(c * CW, CW), CW)
+                xb = (th[:, cs] - mu_ref[:, cs]).astype(BF16)
+                qacc[...] += lax.dot_general(ut_ref[:, cs], xb, NT, preferred_element_type=F32)
+                return carry
+            qacc[...] = jnp.zeros_like(qacc)
+            lax.fori_loop(0, NC, body, 0)
 
         def load_phase(b):
             def body(c, carry):
                 load_th(b, c).wait()
+                if b == 0:
+                    load_a(0, c).start()
                 for i in range(CW // SW):
                     cs = pl.ds(pl.multiple_of(c * CW + i * SW, SW), SW)
                     t = th[b * HB:(b + 1) * HB, cs]
                     new_block(b)[:, cs] = t.astype(BF16)
-                    project(b, cs, (t - mu_ref[:, cs]).astype(BF16))
                 return carry
             lax.fori_loop(0, NC, body, 0)
 
         def update_phase(b):
             def body(c, carry):
                 if b == 1:
-                    at(c == 1, (stage_b, 4))
-                    at(c == 2, (stage_c, 0))
+                    at(c == 1, (stage_b, 1))
+                    at(c == 3, (stage_c, 0))
                 kb = kx[b * HB:(b + 1) * HB, 0:N]
                 kt = kx[b * HB:(b + 1) * HB, N:2 * N]
                 kvb = kv[b * HB:(b + 1) * HB, 0:1]
@@ -200,7 +205,6 @@
                     t = t + gain * (move + kvb * t)
                     th[b * HB:(b + 1) * HB, cs] = t
                     new_block(b)[:, cs] = t.astype(BF16)
-                    project(b, cs, (t - mu_ref[:, cs]).astype(BF16))
                 return carry
             lax.fori_loop(0, NC, body, 0)
 
@@ -217,17 +221,12 @@
                 row = jnp.sum(jnp.where(eye, g, 0.0), axis=0, keepdims=True)
                 dall[me, :, b * HB:(b + 1) * HB] = jnp.broadcast_to(row, (8, HB))
 
-        def first_gram():
-            gram(0, 0)
-            stage_a(4)
-            stage_b(1)
-
-        qacc[...] = jnp.zeros_like(qacc)
-
         @pl.when(s == 0)
         def _():
             load_phase(0)
-            load_a(0).wait()
+            for c in range(4):
+                load_a(0, c).wait()
+                load_a(1, c).start()
 
         @pl.when(s > 0)
         def _():
@@ -237,49 +236,50 @@
 
         @pl.when(s == 0)
         def _():
-            load_a(1).wait()
+            for c in range(4):
+                load_a(1, c).wait()
+                load_th(1, c).start()
         logits(0, 1)
         stage_b(0)
 
         @pl.when(s == 0)
         def _():
-            first_gram()
             load_phase(1)
-            stage_b(4)
+            stage_b(1)
 
         @pl.when(s > 0)
         def _():
-            first_gram()
             update_phase(1)
-            stage_c(1)
-
+
+        @pl.when(s == NUM_STEPS - 1)
+        def _():
+            out_theta().start()
+
+        @pl.when(s < NUM_STEPS - 1)
+        def _():
+            keep_block0().start()
+
+        logits(1, 0)
+        at(s == 0, (stage_c, 0))
+        at(s > 0, (stage_c, 1), (stage_d, 0))
+        logits(1, 1)
+        at(s == 0, (stage_c, 1))
+        stage_b(2)
+        project()
         qall[me] = qacc[...]
         for p in range(3):
             small_q(p).start()
-
-        @pl.when(s == NUM_STEPS - 1)
-        def _():
-            out_theta().start()
-
-        @pl.when(s < NUM_STEPS - 1)
-        def _():
-            keep_block0().start()
-
-        logits(1, 0)
-        at(s == 0, (stage_c, 0))
-        at(s > 0, (stage_d, 0))
-        logits(1, 1)
-        at(s == 0, (stage_c, 1))
-        at(s > 0, (stage_d, 1))
-        stage_b(2)
         gram(1, 0)
         at(s == 0, (stage_d, 0))
+        at(s > 0, (stage_d, 1))
         gram(1, 1)
         stage_a(5)
+        stage_c(2)
+        at(s == 0, (stage_d, 1))
+        gram(0, 0)
+        stage_a(4)
         for p in range(3):
             small_g(p).start()
-        stage_b(3)
-        at(s == 0, (stage_d, 1))
         stage_e(0)
         stage_e(1)
         for p in range(3):
@@ -306,14 +306,13 @@
             def _():
                 out_s(b).start()
 
-        score_phase(0, {1: [(stage_c, 2)], 2: [(stage_c, 4)], 3: [(stage_c, 3), (stage_b, 5)]})
-        for idx in (2, 3, 4):
-            stage_d(idx)
+        score_phase(0, {1: [(stage_c, 3)], 2: [(stage_d, 2), (stage_b, 5)], 3: [(stage_b, 4), (stage_d, 3)]})
         stage_e(2)
         stage_e(3)
-        score_phase(1, {2: [(stage_c, 5)]})
+        score_phase(1, {1: [(stage_c, 5)], 2: [(stage_c, 4)]})
+        stage_d(5)
+        stage_d(4)
         stage_e(4)
-        stage_d(5)
         for p in range(3):
             small_k(p).wait_recv()
         ksum = (kall[0] + kall[1]) + (kall[2] + kall[3])
@@ -343,13 +342,46 @@
     out_s(1).wait()
 
 
-def last_kernel(gain, kx, kv, s, th, out):
-    for i in range(s.shape[1] // 512):
-        cs = slice(i * 512, (i + 1) * 512)
+def last_kernel(gain, kx_hbm, kv_hbm, s_hbm, th_hbm, out_hbm, kx, kv, s, th, k_sem, s_sem, th_sem, out_sem):
+    blocks = D // LW
+
+    def copy(src, dst, sem, c):
+        cs = pl.ds(pl.multiple_of(c * LW, LW), LW)
+        return pltpu.make_async_copy(src.at[:, cs], dst.at[:, cs], sem.at[c])
+
+    def fetch(c):
+        copy(s_hbm, s, s_sem, c).start()
+        copy(th_hbm, th, th_sem, c).start()
+
+    k_copy = pltpu.make_async_copy(kx_hbm, kx, k_sem.at[0])
+    kv_copy = pltpu.make_async_copy(kv_hbm, kv, k_sem.at[1])
+    k_copy.start()
+    kv_copy.start()
+    for c in range(AHEAD):
+        fetch(c)
+    k_copy.wait()
+    kv_copy.wait()
+
+    def body(c, carry):
+        copy(s_hbm, s, s_sem, c).wait()
+        copy(th_hbm, th, th_sem, c).wait()
+
+        @pl.when(c + AHEAD < blocks)
+        def _():
+            fetch(c + AHEAD)
+        cs = pl.ds(pl.multiple_of(c * LW, LW), LW)
         t = th[:, cs]
         move = (jnp.dot(kx[:, 0:N], s[:, cs], preferred_element_type=F32)
                 + jnp.dot(kx[:, N:2 * N], t.astype(BF16), preferred_element_type=F32))
-        out[:, cs] = t + gain * (move + kv[:, 0:1] * t)
+        th[:, cs] = t + gain * (move + kv[:, 0:1] * t)
+        copy(th, out_hbm, out_sem, c).start()
+        return carry
+    lax.fori_loop(0, blocks, body, 0)
+
+    def drain(c, carry):
+        copy(th, out_hbm, out_sem, c).wait()
+        return carry
+    lax.fori_loop(0, blocks, drain, 0)
 
 
 def solution(mesh):
@@ -376,21 +408,22 @@
                 pltpu.VMEM((6, 64, 512), F32), pltpu.VMEM((N, M), BF16), pltpu.VMEM((N, 2 * N), BF16),
                 pltpu.VMEM((N, 128), F32), pltpu.VMEM((16, N), F32), pltpu.VMEM((4, 16, N), F32),
                 pltpu.VMEM((4, 8, N), F32), pltpu.VMEM((4, 8, N), F32), pltpu.VMEM((N, 128), F32),
-                dma((8,)), dma((2,)), dma((5,)), dma((1,)),
+                dma((8,)), dma((8,)), dma((5,)), dma((1,)),
                 dma((6,)), dma((6,)), dma((6,)), dma((6,)), dma((6,)), dma((6,)), dma((6,)), dma((6,)),
                 dma((3,)), dma((3,)), dma((3,)), dma((3,)), dma((3,)), dma((3,)),
             ],
             compiler_params=pltpu.CompilerParams(
                 collective_id=0, has_side_effects=True, vmem_limit_bytes=VMEM_LIMIT),
         )(particles, prec_diag[None, :], low_factor.T, prior_mean[None, :], data_mat, targets)
-        width = 1024
         return pl.pallas_call(
             functools.partial(last_kernel, consts[3]),
-            grid=(D // width,),
             out_shape=jax.ShapeDtypeStruct((N, D), F32),
-            in_specs=[pl.BlockSpec((N, 2 * N), lambda i: (0, 0)), pl.BlockSpec((N, 128), lambda i: (0, 0)),
-                      pl.BlockSpec((N, width), lambda i: (0, i)), pl.BlockSpec((N, width), lambda i: (0, i))],
-            out_specs=pl.BlockSpec((N, width), lambda i: (0, i)),
+            in_specs=[anyspace] * 4,
+            out_specs=anyspace,
+            scratch_shapes=[
+                pltpu.VMEM((N, 2 * N), BF16), pltpu.VMEM((N, 128), F32), pltpu.VMEM((N, D), BF16), pltpu.VMEM((N, D), F32),
+                dma((2,)), dma((D // LW,)), dma((D // LW,)), dma((D // LW,)),
+            ],
             compiler_params=pltpu.CompilerParams(vmem_limit_bytes=VMEM_LIMIT),
         )(k2, kv2, s2, th2)
 

time: 174 us -> 158 us (0.908)
  Pallas kernels: 174 us -> 157 us
    pallas_call x1, Pallas kernels: 153 us -> 141 us  [local_run(): pl.pallas_call(functools.partial(run_kernel, consts), out_shape=(jax.Shap...]
    pallas_call x1, Pallas kernels: 20.6 us -> 16.1 us  [local_run(): pl.pallas_call(functools.partial(last_kernel, consts[3]), out_shape=jax.S...]
where the time goes in v3:
time: 158 us
  Pallas kernels  157 us (99%)
    pallas_call x1, Pallas kernels, local_run(): pl.pallas_call(functools.partial(run_kernel, consts), out_shape=(jax.Shap...  141 us
    pallas_call x1, Pallas kernels, local_run(): pl.pallas_call(functools.partial(last_kernel, consts[3]), out_shape=jax.S...  16.1 us

profile of v3, /device:TPU:0, one launch (start us, length us, event | category | flops | bytes accessed | tf_op | source)
XLA Modules:
  0.0 157.5 jit_solution(13481184387150414135)
XLA Ops:
  0.0 141.4 %shard_map.64 = (f32[512,8192]{1,0:T(8,128)}, bf16[512,8192]{1,0:T(8,128)(2,1)}, bf16[512,1024]{1,0:T(8,128)(2,1)}, f32[512,128]{1,0:T(8,128)}) custom-call(f32[512,8192]{1,0:T(8,128)} %th_hbm.1, f32[1,8192]{1,0:T(1,128)} %bitcast.5, bf16[16,8192]{1,0:T(8,128)(2,1)} %bitcast.4, f32[1,8192]{1,0:T(1,128)} %bitcast.6, bf16[1024,8192]{1,0:T(8,128)(2,1)} %a_hbm.1, ...), custom_call_target="tpu_custom_call" | custom-call | tf_op jit(solution)/shard_map/pallas_call | solution.py:398
  141.5 16.1 %shard_map.65 = f32[512,8192]{1,0:T(8,128)} custom-call(bf16[512,1024]{1,0:T(8,128)(2,1)} %get-tuple-element.9.kx_hbm, f32[512,128]{1,0:T(8,128)} %get-tuple-element.10.kv_hbm, bf16[512,8192]{1,0:T(8,128)(2,1)} %get-tuple-element.11.s_hbm, f32[512,8192]{1,0:T(8,128)} %get-tuple-element.12.th_hbm), custom_call_target="tpu_custom_call" | custom-call | tf_op jit(solution)/shard_map/pallas_call | solution.py:418

commit v4 on v3

--- a/solution.py
+++ b/solution.py
@@ -189,7 +189,7 @@
                 return carry
             lax.fori_loop(0, NC, body, 0)
 
-        def update_phase(b):
+        def update_phase(b, cw):
             def body(c, carry):
                 if b == 1:
                     at(c == 1, (stage_b, 1))
@@ -197,8 +197,8 @@
                 kb = kx[b * HB:(b + 1) * HB, 0:N]
                 kt = kx[b * HB:(b + 1) * HB, N:2 * N]
                 kvb = kv[b * HB:(b + 1) * HB, 0:1]
-                for i in range(CW // SW):
-                    cs = pl.ds(pl.multiple_of(c * CW + i * SW, SW), SW)
+                for i in range(cw // SW):
+                    cs = pl.ds(pl.multiple_of(c * cw + i * SW, SW), SW)
                     move = (jnp.dot(kb, sbuf[:, cs], preferred_element_type=F32)
                             + jnp.dot(kt, tb[:, cs], preferred_element_type=F32))
                     t = th[b * HB:(b + 1) * HB, cs]
@@ -206,7 +206,7 @@
                     th[b * HB:(b + 1) * HB, cs] = t
                     new_block(b)[:, cs] = t.astype(BF16)
                 return carry
-            lax.fori_loop(0, NC, body, 0)
+            lax.fori_loop(0, D // cw, body, 0)
 
         def logits(b, j):
             zbuf[2 * b + j] = lax.dot_general(
@@ -224,13 +224,14 @@
         @pl.when(s == 0)
         def _():
             load_phase(0)
+            gram(0, 0)
             for c in range(4):
                 load_a(0, c).wait()
                 load_a(1, c).start()
 
         @pl.when(s > 0)
         def _():
-            update_phase(0)
+            update_phase(0, 4096)
 
         logits(0, 0)
 
@@ -249,7 +250,7 @@
 
         @pl.when(s > 0)
         def _():
-            update_phase(1)
+            update_phase(1, 2048)
 
         @pl.when(s == NUM_STEPS - 1)
         def _():
@@ -276,7 +277,10 @@
         stage_a(5)
         stage_c(2)
         at(s == 0, (stage_d, 1))
-        gram(0, 0)
+
+        @pl.when(s > 0)
+        def _():
+            gram(0, 0)
         stage_a(4)
         for p in range(3):
             small_g(p).start()
@@ -288,36 +292,31 @@
         qt[...] = jnp.concatenate([qsum, jnp.zeros((112, N), F32)], axis=0).T
 
         def score_phase(b, events):
-            def body(c, carry):
-                for when, todo in events.items():
-                    at(c == when, *todo)
-                rr = rbuf[b * HB:(b + 1) * HB, :]
-                qb = qt[b * HB:(b + 1) * HB, 0:16].astype(BF16)
-                for i in range(CW // SS):
-                    cs = pl.ds(pl.multiple_of(c * CW + i * SS, SS), SS)
-                    lik = jnp.dot(rr, a[:, cs], preferred_element_type=F32)
-                    low = jnp.dot(qb, ut_ref[:, cs], preferred_element_type=F32)
-                    x = th[b * HB:(b + 1) * HB, cs] - mu_ref[:, cs]
-                    sbuf[b * HB:(b + 1) * HB, cs] = (lik_weight * lik - x * lam_ref[:, cs] - low).astype(BF16)
-                return carry
-            lax.fori_loop(0, NC, body, 0)
+            rr = rbuf.at[pl.ds(b * HB, HB), :]
+            qb = qt.at[pl.ds(b * HB, HB), pl.ds(0, 128)]
+            for i in range(D // SS):
+                for f, idx in events.get(i, ()):
+                    f(idx)
+                cs = slice(i * SS, (i + 1) * SS)
+                lik = jnp.dot(rr[...], a[:, cs], preferred_element_type=F32)
+                low = jnp.dot(qb[:, 0:16].astype(BF16), ut_ref[:, cs], preferred_element_type=F32)
+                x = th[b * HB:(b + 1) * HB, cs] - mu_ref[:, cs]
+                sbuf[b * HB:(b + 1) * HB, cs] = (lik_weight * lik - x * lam_ref[:, cs] - low).astype(BF16)
 
             @pl.when(s == NUM_STEPS - 1)
             def _():
                 out_s(b).start()
 
-        score_phase(0, {1: [(stage_c, 3)], 2: [(stage_d, 2), (stage_b, 5)], 3: [(stage_b, 4), (stage_d, 3)]})
+        score_phase(0, {3: [(stage_c, 3)], 6: [(stage_d, 2), (stage_b, 5)], 7: [(stage_b, 4)], 12: [(stage_d, 3)]})
         stage_e(2)
         stage_e(3)
-        score_phase(1, {1: [(stage_c, 5)], 2: [(stage_c, 4)]})
-        stage_d(5)
-        stage_d(4)
+        score_phase(1, {3: [(stage_c, 5)], 6: [(stage_c, 4)], 12: [(stage_d, 5)], 14: [(stage_d, 4)]})
+        stage_e(5)
         stage_e(4)
         for p in range(3):
             small_k(p).wait_recv()
         ksum = (kall[0] + kall[1]) + (kall[2] + kall[3])
         kv[...] = jnp.broadcast_to(two_over_band * ksum[0:1, :], (128, N)).T
-        stage_e(5)
         kx[0:HB, HB:N] = kx[HB:N, 0:HB].astype(F32).T.astype(BF16)
         kx[:, N:2 * N] = (kx[:, 0:N].astype(F32) * -two_over_band).astype(BF16)
         for p in range(3):

time: 158 us -> 154 us (0.975)
  Pallas kernels: 157 us -> 154 us
    pallas_call x1, Pallas kernels: 141 us -> 138 us  [local_run(): pl.pallas_call(functools.partial(run_kernel, consts), out_shape=(jax.Shap...]
where the time goes in v4:
time: 154 us
  Pallas kernels  154 us (100%)
    pallas_call x1, Pallas kernels, local_run(): pl.pallas_call(functools.partial(run_kernel, consts), out_shape=(jax.Shap...  138 us
    pallas_call x1, Pallas kernels, local_run(): pl.pallas_call(functools.partial(last_kernel, consts[3]), out_shape=jax.S...  16.1 us

profile of v4, /device:TPU:0, one launch (start us, length us, event | category | flops | bytes accessed | tf_op | source)
XLA Modules:
  0.0 153.7 jit_solution(15618427994944983011)
XLA Ops:
  0.0 137.6 %shard_map.64 = (f32[512,8192]{1,0:T(8,128)}, bf16[512,8192]{1,0:T(8,128)(2,1)}, bf16[512,1024]{1,0:T(8,128)(2,1)}, f32[512,128]{1,0:T(8,128)}) custom-call(f32[512,8192]{1,0:T(8,128)} %th_hbm.1, f32[1,8192]{1,0:T(1,128)} %bitcast.5, bf16[16,8192]{1,0:T(8,128)(2,1)} %bitcast.4, f32[1,8192]{1,0:T(1,128)} %bitcast.6, bf16[1024,8192]{1,0:T(8,128)(2,1)} %a_hbm.1, ...), custom_call_target="tpu_custom_call" | custom-call | tf_op jit(solution)/shard_map/pallas_call | solution.py:397
  137.6 16.1 %shard_map.65 = f32[512,8192]{1,0:T(8,128)} custom-call(bf16[512,1024]{1,0:T(8,128)(2,1)} %get-tuple-element.9.kx_hbm, f32[512,128]{1,0:T(8,128)} %get-tuple-element.10.kv_hbm, bf16[512,8192]{1,0:T(8,128)(2,1)} %get-tuple-element.11.s_hbm, f32[512,8192]{1,0:T(8,128)} %get-tuple-element.12.th_hbm), custom_call_target="tpu_custom_call" | custom-call | tf_op jit(solution)/shard_map/pallas_call | solution.py:417

commit v5 on v4

--- a/solution.py
+++ b/solution.py
@@ -169,13 +169,13 @@
 
         def project():
             def body(c, carry):
-                at(c == 2, (stage_b, 3))
-                cs = pl.ds(pl.multiple_of(c * CW, CW), CW)
+                at(c == 1, (stage_b, 3))
+                cs = pl.ds(pl.multiple_of(c * (2 * CW), CW), 2 * CW)
                 xb = (th[:, cs] - mu_ref[:, cs]).astype(BF16)
                 qacc[...] += lax.dot_general(ut_ref[:, cs], xb, NT, preferred_element_type=F32)
                 return carry
             qacc[...] = jnp.zeros_like(qacc)
-            lax.fori_loop(0, NC, body, 0)
+            lax.fori_loop(0, NC // 2, body, 0)
 
         def load_phase(b):
             def body(c, carry):
@@ -189,24 +189,28 @@
                 return carry
             lax.fori_loop(0, NC, body, 0)
 
-        def update_phase(b, cw):
-            def body(c, carry):
-                if b == 1:
-                    at(c == 1, (stage_b, 1))
-                    at(c == 3, (stage_c, 0))
-                kb = kx[b * HB:(b + 1) * HB, 0:N]
-                kt = kx[b * HB:(b + 1) * HB, N:2 * N]
-                kvb = kv[b * HB:(b + 1) * HB, 0:1]
-                for i in range(cw // SW):
-                    cs = pl.ds(pl.multiple_of(c * cw + i * SW, SW), SW)
-                    move = (jnp.dot(kb, sbuf[:, cs], preferred_element_type=F32)
-                            + jnp.dot(kt, tb[:, cs], preferred_element_type=F32))
-                    t = th[b * HB:(b + 1) * HB, cs]
-                    t = t + gain * (move + kvb * t)
-                    th[b * HB:(b + 1) * HB, cs] = t
-                    new_block(b)[:, cs] = t.astype(BF16)
-                return carry
-            lax.fori_loop(0, D // cw, body, 0)
+        def update_columns(b, cs):
+            move = (jnp.dot(kx[b * HB:(b + 1) * HB, 0:N], sbuf[:, cs], preferred_element_type=F32)
+                    + jnp.dot(kx[b * HB:(b + 1) * HB, N:2 * N], tb[:, cs], preferred_element_type=F32))
+            t = th[b * HB:(b + 1) * HB, cs]
+            t = t + gain * (move + kv[b * HB:(b + 1) * HB, 0:1] * t)
+            th[b * HB:(b + 1) * HB, cs] = t
+            new_block(b)[:, cs] = t.astype(BF16)
+
+        def update_phase(b):
+            if b == 0:
+                def body(c, carry):
+                    for i in range(4):
+                        update_columns(b, pl.ds(pl.multiple_of(c * 4 * SW + i * SW, SW), SW))
+                    return carry
+                lax.fori_loop(0, D // (4 * SW), body, 0)
+            else:
+                for i in range(D // SW):
+                    if i == 2:
+                        stage_b(1)
+                    if i == 6:
+                        stage_c(0)
+                    update_columns(b, slice(i * SW, (i + 1) * SW))
 
         def logits(b, j):
             zbuf[2 * b + j] = lax.dot_general(
@@ -231,7 +235,7 @@
 
         @pl.when(s > 0)
         def _():
-            update_phase(0, 4096)
+            update_phase(0)
 
         logits(0, 0)
 
@@ -250,7 +254,7 @@
 
         @pl.when(s > 0)
         def _():
-            update_phase(1, 2048)
+            update_phase(1)
 
         @pl.when(s == NUM_STEPS - 1)
         def _():

time: 154 us -> 153 us (level)
  no operation moved by 1% of the time
where the time goes in v5:
time: 153 us
  Pallas kernels  153 us (100%)
    pallas_call x1, Pallas kernels, local_run(): pl.pallas_call(functools.partial(run_kernel, consts), out_shape=(jax.Shap...  137 us
    pallas_call x1, Pallas kernels, local_run(): pl.pallas_call(functools.partial(last_kernel, consts[3]), out_shape=jax.S...  16.1 us

profile of v5, /device:TPU:0, one launch (start us, length us, event | category | flops | bytes accessed | tf_op | source)
XLA Modules:
  0.0 153.2 jit_solution(74407685209476267)
XLA Ops:
  0.0 137.1 %shard_map.64 = (f32[512,8192]{1,0:T(8,128)}, bf16[512,8192]{1,0:T(8,128)(2,1)}, bf16[512,1024]{1,0:T(8,128)(2,1)}, f32[512,128]{1,0:T(8,128)}) custom-call(f32[512,8192]{1,0:T(8,128)} %th_hbm.1, f32[1,8192]{1,0:T(1,128)} %bitcast.5, bf16[16,8192]{1,0:T(8,128)(2,1)} %bitcast.4, f32[1,8192]{1,0:T(1,128)} %bitcast.6, bf16[1024,8192]{1,0:T(8,128)(2,1)} %a_hbm.1, ...), custom_call_target="tpu_custom_call" | custom-call | tf_op jit(solution)/shard_map/pallas_call | solution.py:401
  137.1 16.1 %shard_map.65 = f32[512,8192]{1,0:T(8,128)} custom-call(bf16[512,1024]{1,0:T(8,128)(2,1)} %get-tuple-element.9.kx_hbm, f32[512,128]{1,0:T(8,128)} %get-tuple-element.10.kv_hbm, bf16[512,8192]{1,0:T(8,128)(2,1)} %get-tuple-element.11.s_hbm, f32[512,8192]{1,0:T(8,128)} %get-tuple-element.12.th_hbm), custom_call_target="tpu_custom_call" | custom-call | tf_op jit(solution)/shard_map/pallas_call | solution.py:421
